TPU v7x, 32 devices: a whole 2x2x4 slice. The times are simulated.
32 devices in a mesh: dom: 8 (over z, y), level: 4 (over x, core).
Axes of the slice: x: 2, y: 2, z: 4, core: 2. Of those that a mesh axis runs over, the one named last changes fastest.
Arguments:
- dg_values: bfloat16 [98304, 384], P(('dom', 'level')), may hold values from -6 to 6
- stiff_mu: bfloat16 [384, 384], replicated, may hold values from -0.1 to 2, as said below
- stiff_lam: bfloat16 [384, 384], replicated, may hold values from -0.1 to 2, as said below
- coef_mu: float32 [98304], P(('dom', 'level')), may hold values from 0.25 to 4
- coef_lam: float32 [98304], P(('dom', 'level')), may hold values from 0.25 to 4
- elem_count: int32 [32], P(('dom', 'level')), may hold values from 384 to 3072, as said below
- elem_block: int32 [3, 98304], P(None, ('dom', 'level')), may hold values from 0 to 1023
- share_map: int32 [32, 8, 32], P(('dom', 'level')), may hold values from 0 to 1024, as said below
- hang_child: int32 [32, 64], P(('dom', 'level')), may hold values from 0 to 1024, as said below
- hang_parent: int32 [32, 64, 2], P(('dom', 'level')), may hold values from 0 to 1023
Outputs:
- projected: float32 [3, 32768, 128], P(None, ('dom', 'level'))
- energy: float32 [], replicated
Inputs may be any that keep to these rules, and one draw needn't show every extreme that they name: `elem_count`: between 384 and 3072; one device, drawn anew, holds exactly 3072. `share_map`: Slots agree in pairs: [d, o, s] is live exactly when the partner's [d2, o', s] is live, and they name the same DoF block. Slots toward ranks outside 0 to 7 are empty. For every offset some rank pair fills all 32 slots. `hang_child`: on each device of level index 1 or more, 64 distinct blocks below 1024; on devices of level index 0 every entry is 1024 (no hanging blocks). `hang_parent`: block numbers on the device of the same rank and the next lower level index; unused on level index 0. `stiff_mu`: Symmetric. `stiff_lam`: Symmetric.
All inputs are finite; a program needn't handle non-finite values.
Results may differ from a plain program's by a relative error of at most 0.0003.
Values sent between devices are 32-bit elements; how exact they have to be, the bound alone decides.
A program may use at most 64 MiB of HBM per device.

v0:
```python
import jax
import jax.numpy as jnp
from jax import lax
from jax.sharding import PartitionSpec as P


def from_behind(block, axis, distance):
    devices = range(lax.axis_size(axis))
    route = [(i - distance, i) for i in devices if i - distance in devices]
    return lax.ppermute(block, axis, route)


def shards(
    dg_values,
    stiff_mu,
    stiff_lam,
    coef_mu,
    coef_lam,
    elem_count,
    elem_block,
    share_map,
    hang_child,
    hang_parent,
):
    elements = dg_values.shape[0]
    row_width = stiff_mu.shape[0]
    block_size = row_width // 3
    block_count = elements // 3
    offsets_half = share_map.shape[1] // 2
    joined = jnp.concatenate((stiff_mu, stiff_lam), axis=1)
    product = jnp.dot(dg_values, joined, preferred_element_type=jnp.float32)
    forces = coef_mu[:, None] * product[:, :row_width] + coef_lam[:, None] * product[:, row_width:]
    live_rows = jnp.arange(elements) < elem_count[0]
    forces = jnp.where(live_rows[:, None], forces, jnp.float32(0.0))
    energy_part = 0.5 * jnp.sum(dg_values.astype(jnp.float32) * forces)
    component_forces = jnp.transpose(forces.reshape(elements, 3, block_size), (1, 0, 2))
    block_ids = jnp.arange(block_count + 1, dtype=jnp.int32)

    def sum_blocks(packed):
        target_ids, component_part = packed
        selector = (block_ids[:, None] == target_ids[None, :]).astype(jnp.float32)
        return jnp.dot(
            selector,
            component_part,
            precision=lax.Precision.HIGHEST,
            preferred_element_type=jnp.float32,
        )

    local_blocks = lax.map(sum_blocks, (elem_block, component_forces))
    slot_blocks = share_map[0]
    outgoing = jnp.transpose(local_blocks[:, slot_blocks, :], (1, 0, 2, 3))
    offsets = [step + 1 for step in range(offsets_half)] + [
        -(step + 1) for step in range(offsets_half)
    ]
    pieces = [None] * (2 * offsets_half)
    for slot_index in range(2 * offsets_half):
        opposite = (slot_index + offsets_half) % (2 * offsets_half)
        pieces[opposite] = from_behind(outgoing[slot_index], "dom", offsets[slot_index])
    incoming = jnp.stack(pieces)
    received = jnp.transpose(incoming, (1, 0, 2, 3)).reshape(3, -1, block_size)
    assembled = local_blocks.at[:, slot_blocks.reshape(-1), :].add(received)
    wanted = from_behind(hang_parent, "level", -1)
    chosen = assembled[:, wanted[0].reshape(-1), :]
    picked = from_behind(chosen, "level", 1)
    parent_pairs = picked.reshape(3, -1, 2, block_size)
    child_values = 0.5 * (parent_pairs[:, :, 0] + parent_pairs[:, :, 1])
    projected = assembled.at[:, hang_child[0], :].set(child_values)
    scale_total = jnp.float32(row_width * elements * lax.axis_size("dom") * lax.axis_size("level"))
    energy = lax.psum(energy_part, ("dom", "level")) / scale_total
    return (projected[:, :block_count], energy)


def solution(mesh):
    return jax.shard_map(
        shards,
        mesh=mesh,
        in_specs=(
            P(("dom", "level"), None),
            P(),
            P(),
            P(("dom", "level")),
            P(("dom", "level")),
            P(("dom", "level")),
            P(None, ("dom", "level")),
            P(("dom", "level"), None, None),
            P(("dom", "level"), None),
            P(("dom", "level"), None, None),
        ),
        out_specs=(P(None, ("dom", "level"), None), P()),
        check_vma=False,
    )
```

profile of v0, /device:TPU:18, one launch (start us, length us, event | category | flops | bytes accessed | tf_op | source)
XLA Modules:
  0.0 186.4 jit_solution(15404276880878706162)
XLA Ops:
  2.6 4.4 %copy.33 = bf16[3072,384]{0,1:T(8,128)(2,1)} copy(bf16[3072,384]{1,0:T(8,128)(2,1)} %param.12) | data formatting | bytes 4718592 | tf_op args[0]
  7.8 2.7 %convolution_bitcast_fusion = f32[3072,768]{0,1:T(8,128)S(1)} fusion(bf16[3072,384]{1,0:T(8,128)(2,1)S(1)} %copy-done, bf16[384,384]{1,0:T(8,128)(2,1)S(1)} %copy-done.3, bf16[384,384]{1,0:T(8,128)(2,1)S(1)} %copy-done.4), kind=kOutput, calls=%fused_computation.13 | convolution fusion | flops 1813118976 | bytes 12386304 | tf_op jit(solution)/shard_map/dot_general | solution.py:31
  10.4 4.5 %multiply_reduce_fusion = (f32[]{:T(128)}, f32[3072,384]{0,1:T(8,128)}) fusion(bf16[3072,384]{0,1:T(8,128)(2,1)S(1)} %copy-done.1, f32[3072,768]{0,1:T(8,128)S(1)} %convolution_bitcast_fusion, f32[3072]{0:T(1024)S(1)} %copy-done.6, f32[3072]{0:T(1024)S(1)} %copy-done.7, pred[3072]{0:T(1024)(128)(4,1)S(1)} %iota_compare_fusion.4), kind=kLoop, calls=%fused_computation.18 | loop fusion | flops 8257535 | bytes 16542724 | tf_op jit(solution)/shard_map/reduce_sum | solution.py:35
  14.9 6.2 %copy.27 = f32[3072,3,128]{2,0,1:T(8,128)} copy(f32[3072,3,128]{0,2,1:T(8,128)} %bitcast.88) | data formatting | bytes 9437184 | tf_op jit(solution)/shard_map/reshape | solution.py:36
  21.1 73.7 %while.11 = (s32[]{:T(128)}, f32[3,1025,128]{2,0,1:T(4,128)S(1)}, s32[3,3072]{1,0:T(4,128)}, f32[3,3072,128]{2,1,0:T(8,128)}, s32[]{:T(128)}, /*index=5*/s32[]{:T(128)}) while((s32[]{:T(128)}, f32[3,1025,128]{2,0,1:T(4,128)S(1)}, s32[3,3072]{1,0:T(4,128)}, f32[3,3072,128]{2,1,0:T(8,128)}, s32[]{:T(128)}, /*index=5*/s32[]{:T(128)}) %tuple.40), condition=%wide.region_1.2_spmd.clone, body=%wide.region_0.1_spmd.clone.sunk | while | flops 4839705600 | bytes 4234317 | solution.py:49
  21.9 7.2 %fusion.24 = f32[1,1025,128]{2,1,0:T(8,128)S(1)} fusion(s32[3072]{0:T(1024)S(1)} %bitcast.92, f32[3,3072,128]{2,1,0:T(8,128)} %get-tuple-element.104, s32[]{:T(128)} %get-tuple-element.95), kind=kOutput, calls=%fused_computation.8.clone.1 | convolution fusion | flops 4839705600 | bytes 2110464 | tf_op jit(solution)/shard_map/while/body/eval_jaxpr/dot_general | solution.py:42
  29.1 3.3 %copy.41 = f32[1,1025,128]{2,0,1:T(1,128)S(1)} copy(f32[1,1025,128]{2,1,0:T(8,128)S(1)} %fusion.24) | data formatting | bytes 1049600 | tf_op jit(solution)/shard_map/while/body/jit(dynamic_update_index_in_dim)/dynamic_update_slice | solution.py:49
  32.4 13.2 %dynamic_update_slice.6 = f32[3,1025,128]{2,0,1:T(4,128)S(1)} dynamic-update-slice(f32[3,1025,128]{2,0,1:T(4,128)S(1)} %get-tuple-element.96, f32[1,1025,128]{2,0,1:T(1,128)S(1)} %copy.41, s32[]{:T(128)} %get-tuple-element.95, s32[]{:T(128)} %constant.11.clone.1..sunk, s32[]{:T(128)} %constant.11.clone.1..sunk) | dynamic-update-slice | bytes 1049604 | tf_op jit(solution)/shard_map/while/body/jit(dynamic_update_index_in_dim)/dynamic_update_slice | solution.py:49
  46.5 7.2 %fusion.24 = f32[1,1025,128]{2,1,0:T(8,128)S(1)} fusion(s32[3072]{0:T(1024)S(1)} %bitcast.92, f32[3,3072,128]{2,1,0:T(8,128)} %get-tuple-element.104, s32[]{:T(128)} %get-tuple-element.95), kind=kOutput, calls=%fused_computation.8.clone.1 | convolution fusion | flops 4839705600 | bytes 2110464 | tf_op jit(solution)/shard_map/while/body/eval_jaxpr/dot_general | solution.py:42
  53.7 3.3 %copy.41 = f32[1,1025,128]{2,0,1:T(1,128)S(1)} copy(f32[1,1025,128]{2,1,0:T(8,128)S(1)} %fusion.24) | data formatting | bytes 1049600 | tf_op jit(solution)/shard_map/while/body/jit(dynamic_update_index_in_dim)/dynamic_update_slice | solution.py:49
  57.0 13.2 %dynamic_update_slice.6 = f32[3,1025,128]{2,0,1:T(4,128)S(1)} dynamic-update-slice(f32[3,1025,128]{2,0,1:T(4,128)S(1)} %get-tuple-element.96, f32[1,1025,128]{2,0,1:T(1,128)S(1)} %copy.41, s32[]{:T(128)} %get-tuple-element.95, s32[]{:T(128)} %constant.11.clone.1..sunk, s32[]{:T(128)} %constant.11.clone.1..sunk) | dynamic-update-slice | bytes 1049604 | tf_op jit(solution)/shard_map/while/body/jit(dynamic_update_index_in_dim)/dynamic_update_slice | solution.py:49
  71.0 7.2 %fusion.24 = f32[1,1025,128]{2,1,0:T(8,128)S(1)} fusion(s32[3072]{0:T(1024)S(1)} %bitcast.92, f32[3,3072,128]{2,1,0:T(8,128)} %get-tuple-element.104, s32[]{:T(128)} %get-tuple-element.95), kind=kOutput, calls=%fused_computation.8.clone.1 | convolution fusion | flops 4839705600 | bytes 2110464 | tf_op jit(solution)/shard_map/while/body/eval_jaxpr/dot_general | solution.py:42
  78.2 3.3 %copy.41 = f32[1,1025,128]{2,0,1:T(1,128)S(1)} copy(f32[1,1025,128]{2,1,0:T(8,128)S(1)} %fusion.24) | data formatting | bytes 1049600 | tf_op jit(solution)/shard_map/while/body/jit(dynamic_update_index_in_dim)/dynamic_update_slice | solution.py:49
  81.5 13.2 %dynamic_update_slice.6 = f32[3,1025,128]{2,0,1:T(4,128)S(1)} dynamic-update-slice(f32[3,1025,128]{2,0,1:T(4,128)S(1)} %get-tuple-element.96, f32[1,1025,128]{2,0,1:T(1,128)S(1)} %copy.41, s32[]{:T(128)} %get-tuple-element.95, s32[]{:T(128)} %constant.11.clone.1..sunk, s32[]{:T(128)} %constant.11.clone.1..sunk) | dynamic-update-slice | bytes 1049604 | tf_op jit(solution)/shard_map/while/body/jit(dynamic_update_index_in_dim)/dynamic_update_slice | solution.py:49
  97.0 3.3 %collective-permute-start = (f32[3,32,128]{2,0,1:T(4,128)S(1)}, f32[3,32,128]{2,0,1:T(4,128)S(1)}, u32[]{:S(2)}, u32[]{:S(2)}) collective-permute-start(f32[3,32,128]{2,0,1:T(4,128)S(1)} %get-tuple-element.61), channel_id=1, source_target_pairs={{4,0},{8,4},{12,8},{16,12},{20,16},{24,20},{28,24},{5,1},{9,5},{13... | collective-permute-start | bytes 147464 | tf_op jit(solution)/shard_map/ppermute | solution.py:10
  100.3 40.1 %psum.7 = f32[]{:T(128)} all-reduce(f32[]{:T(128)S(6)} %mul.39), channel_id=1, replica_groups=mesh['dom'=8,'level'=4] {'dom','level'}, use_global_device_ids=true, to_apply=%region_5.6 | all-reduce | flops 1 | bytes 8 | tf_op jit(solution)/shard_map/psum | solution.py:69
  141.1 2.5 %collective-permute-start.1 = (f32[3,32,128]{2,0,1:T(4,128)S(1)}, f32[3,32,128]{2,0,1:T(4,128)S(1)}, u32[]{:S(2)}, u32[]{:S(2)}) collective-permute-start(f32[3,32,128]{2,0,1:T(4,128)S(1)} %get-tuple-element.60), channel_id=1, source_target_pairs={{8,0},{12,4},{16,8},{20,12},{24,16},{28,20},{9,1},{13,5},{17,9},{2... | collective-permute-start | bytes 147464 | tf_op jit(solution)/shard_map/ppermute | solution.py:10
  143.7 2.2 %collective-permute-start.2 = (f32[3,32,128]{2,0,1:T(4,128)S(1)}, f32[3,32,128]{2,0,1:T(4,128)S(1)}, u32[]{:S(2)}, u32[]{:S(2)}) collective-permute-start(f32[3,32,128]{2,0,1:T(4,128)S(1)} %get-tuple-element.59), channel_id=1, source_target_pairs={{12,0},{16,4},{20,8},{24,12},{28,16},{13,1},{17,5},{21,9},{25,13},... | collective-permute-start | bytes 147464 | tf_op jit(solution)/shard_map/ppermute | solution.py:10
  147.2 3.6 %collective-permute-start.4 = (f32[3,32,128]{2,0,1:T(4,128)S(1)}, f32[3,32,128]{2,0,1:T(4,128)S(1)}, u32[]{:S(2)}, u32[]{:S(2)}) collective-permute-start(f32[3,32,128]{2,0,1:T(4,128)S(1)} %get-tuple-element.57), channel_id=1, source_target_pairs={{0,4},{4,8},{8,12},{12,16},{16,20},{20,24},{24,28},{1,5},{5,9},{9,... | collective-permute-start | bytes 147464 | tf_op jit(solution)/shard_map/ppermute | solution.py:10
  150.8 4.1 %collective-permute-start.5 = (f32[3,32,128]{2,0,1:T(4,128)S(1)}, f32[3,32,128]{2,0,1:T(4,128)S(1)}, u32[]{:S(2)}, u32[]{:S(2)}) collective-permute-start(f32[3,32,128]{2,0,1:T(4,128)S(1)} %get-tuple-element.56), channel_id=1, source_target_pairs={{0,8},{4,12},{8,16},{12,20},{16,24},{20,28},{1,9},{5,13},{9,17},{1... | collective-permute-start | bytes 147464 | tf_op jit(solution)/shard_map/ppermute | solution.py:10
  158.3 4.7 %collective-permute-done.6 = f32[3,32,128]{2,0,1:T(4,128)S(1)} collective-permute-done((f32[3,32,128]{2,0,1:T(4,128)S(1)}, f32[3,32,128]{2,0,1:T(4,128)S(1)}, u32[]{:S(2)}, u32[]{:S(2)}) %collective-permute-start.6) | collective-permute-done | bytes 49184 | tf_op jit(solution)/shard_map/ppermute | solution.py:10
  163.9 8.8 %scatter_fusion = f32[3,1025,128]{2,0,1:T(4,128)S(1)} fusion(f32[3,1025,128]{2,0,1:T(4,128)S(1)} %get-tuple-element.29, s32[256]{0:T(256)S(1)} %bitcast.95, f32[256,3,128]{2,1,0:T(4,128)S(1)} %bitcast.91), kind=kCustom, calls=%fused_computation.2 | custom fusion | flops 98304 | bytes 1180672 | tf_op jit(solution)/shard_map/scatter-add | solution.py:61
  175.4 5.7 %collective-permute-done.9 = f32[3,128,128]{2,0,1:T(4,128)S(1)} collective-permute-done((f32[3,128,128]{2,0,1:T(4,128)S(1)}, f32[3,128,128]{2,0,1:T(4,128)S(1)}, u32[]{:S(2)}, u32[]{:S(2)}) %collective-permute-start.9) | collective-permute-done | bytes 196640 | tf_op jit(solution)/shard_map/ppermute | solution.py:10
  181.2 2.4 %scatter_fusion.1 = f32[3,1025,128]{2,0,1:T(4,128)S(1)} fusion(f32[3,1025,128]{2,0,1:T(4,128)S(1)} %scatter_fusion, s32[64]{0:T(128)S(1)} %fusion.16, f32[64,3,128]{2,1,0:T(4,128)S(1)} %fusion.15), kind=kCustom, calls=%fused_computation.3 | custom fusion | bytes 295168 | tf_op jit(solution)/shard_map/scatter | solution.py:67
  (59 shorter events, 15.9 us)
Async XLA Ops:
  0.6 95.0 %collective-permute-start.8 = (s32[1,64,2]{1,2,0:T(2,128)}, s32[1,64,2]{1,2,0:T(2,128)S(1)}, u32[]{:S(2)}, u32[]{:S(2)}) collective-permute-start(s32[1,64,2]{1,2,0:T(2,128)} %param.21), channel_id=1, source_target_pairs={{1,0},{2,1},{3,2},{5,4},{6,5},{7,6},{9,8},{10,9},{11,10},{13,12},{... | collective-permute-start | bytes 1544 | tf_op jit(solution)/shard_map/ppermute | solution.py:10
  2.6 5.1 %copy-start = (bf16[3072,384]{1,0:T(8,128)(2,1)S(1)}, bf16[3072,384]{1,0:T(8,128)(2,1)}, u32[]{:S(2)}) copy-start(bf16[3072,384]{1,0:T(8,128)(2,1)} %param.12) | copy-start | bytes 7077892
  2.6 5.1 %copy-start.3 = (bf16[384,384]{1,0:T(8,128)(2,1)S(1)}, bf16[384,384]{1,0:T(8,128)(2,1)}, u32[]{:S(2)}) copy-start(bf16[384,384]{1,0:T(8,128)(2,1)} %param.14) | copy-start | bytes 884740
  2.6 5.1 %copy-start.4 = (bf16[384,384]{1,0:T(8,128)(2,1)S(1)}, bf16[384,384]{1,0:T(8,128)(2,1)}, u32[]{:S(2)}) copy-start(bf16[384,384]{1,0:T(8,128)(2,1)} %param.13) | copy-start | bytes 884740
  7.7 2.7 %copy-start.1 = (bf16[3072,384]{0,1:T(8,128)(2,1)S(1)}, bf16[3072,384]{0,1:T(8,128)(2,1)}, u32[]{:S(2)}) copy-start(bf16[3072,384]{0,1:T(8,128)(2,1)} %copy.33) | copy-start | bytes 7077892
  7.7 2.7 %copy-start.6 = (f32[3072]{0:T(1024)S(1)}, f32[3072]{0:T(1024)}, u32[]{:S(2)}) copy-start(f32[3072]{0:T(1024)} %param.16) | copy-start | bytes 36868
  7.7 2.7 %copy-start.7 = (f32[3072]{0:T(1024)S(1)}, f32[3072]{0:T(1024)}, u32[]{:S(2)}) copy-start(f32[3072]{0:T(1024)} %param.15) | copy-start | bytes 36868
  14.9 6.2 %copy-start.2 = (f32[3,1025,128]{2,0,1:T(4,128)S(1)}, f32[3,1025,128]{2,0,1:T(4,128)}, u32[]{:S(2)}) copy-start(f32[3,1025,128]{2,0,1:T(4,128)} %custom-call.5) | copy-start | bytes 4723204
  21.1 73.7 %copy-start.5 = (s32[1,8,32]{2,1,0:T(8,128)S(1)}, s32[1,8,32]{2,1,0:T(8,128)}, u32[]{:S(2)}) copy-start(s32[1,8,32]{2,1,0:T(8,128)} %param.19) | copy-start | bytes 3076
  94.8 80.6 %copy-start.8 = (s32[1,64]{1,0:T(1,128)S(1)}, s32[1,64]{1,0:T(1,128)}, u32[]{:S(2)}) copy-start(s32[1,64]{1,0:T(1,128)} %param.20) | copy-start | bytes 772
  97.0 53.8 %collective-permute-start = (f32[3,32,128]{2,0,1:T(4,128)S(1)}, f32[3,32,128]{2,0,1:T(4,128)S(1)}, u32[]{:S(2)}, u32[]{:S(2)}) collective-permute-start(f32[3,32,128]{2,0,1:T(4,128)S(1)} %get-tuple-element.61), channel_id=1, source_target_pairs={{4,0},{8,4},{12,8},{16,12},{20,16},{24,20},{28,24},{5,1},{9,5},{13... | collective-permute-start | bytes 147464 | tf_op jit(solution)/shard_map/ppermute | solution.py:10
  141.1 13.8 %collective-permute-start.1 = (f32[3,32,128]{2,0,1:T(4,128)S(1)}, f32[3,32,128]{2,0,1:T(4,128)S(1)}, u32[]{:S(2)}, u32[]{:S(2)}) collective-permute-start(f32[3,32,128]{2,0,1:T(4,128)S(1)} %get-tuple-element.60), channel_id=1, source_target_pairs={{8,0},{12,4},{16,8},{20,12},{24,16},{28,20},{9,1},{13,5},{17,9},{2... | collective-permute-start | bytes 147464 | tf_op jit(solution)/shard_map/ppermute | solution.py:10
  143.7 13.2 %collective-permute-start.2 = (f32[3,32,128]{2,0,1:T(4,128)S(1)}, f32[3,32,128]{2,0,1:T(4,128)S(1)}, u32[]{:S(2)}, u32[]{:S(2)}) collective-permute-start(f32[3,32,128]{2,0,1:T(4,128)S(1)} %get-tuple-element.59), channel_id=1, source_target_pairs={{12,0},{16,4},{20,8},{24,12},{28,16},{13,1},{17,5},{21,9},{25,13},... | collective-permute-start | bytes 147464 | tf_op jit(solution)/shard_map/ppermute | solution.py:10
  145.9 12.3 %collective-permute-start.3 = (f32[3,32,128]{2,0,1:T(4,128)S(1)}, f32[3,32,128]{2,0,1:T(4,128)S(1)}, u32[]{:S(2)}, u32[]{:S(2)}) collective-permute-start(f32[3,32,128]{2,0,1:T(4,128)S(1)} %get-tuple-element.58), channel_id=1, source_target_pairs={{16,0},{20,4},{24,8},{28,12},{17,1},{21,5},{25,9},{29,13},{18,2},{... | collective-permute-start | bytes 147464 | tf_op jit(solution)/shard_map/ppermute | solution.py:10
  147.2 11.0 %collective-permute-start.4 = (f32[3,32,128]{2,0,1:T(4,128)S(1)}, f32[3,32,128]{2,0,1:T(4,128)S(1)}, u32[]{:S(2)}, u32[]{:S(2)}) collective-permute-start(f32[3,32,128]{2,0,1:T(4,128)S(1)} %get-tuple-element.57), channel_id=1, source_target_pairs={{0,4},{4,8},{8,12},{12,16},{16,20},{20,24},{24,28},{1,5},{5,9},{9,... | collective-permute-start | bytes 147464 | tf_op jit(solution)/shard_map/ppermute | solution.py:10
  150.8 7.5 %collective-permute-start.5 = (f32[3,32,128]{2,0,1:T(4,128)S(1)}, f32[3,32,128]{2,0,1:T(4,128)S(1)}, u32[]{:S(2)}, u32[]{:S(2)}) collective-permute-start(f32[3,32,128]{2,0,1:T(4,128)S(1)} %get-tuple-element.56), channel_id=1, source_target_pairs={{0,8},{4,12},{8,16},{12,20},{16,24},{20,28},{1,9},{5,13},{9,17},{1... | collective-permute-start | bytes 147464 | tf_op jit(solution)/shard_map/ppermute | solution.py:10
  154.9 8.1 %collective-permute-start.6 = (f32[3,32,128]{2,0,1:T(4,128)S(1)}, f32[3,32,128]{2,0,1:T(4,128)S(1)}, u32[]{:S(2)}, u32[]{:S(2)}) collective-permute-start(f32[3,32,128]{2,0,1:T(4,128)S(1)} %get-tuple-element.55), channel_id=1, source_target_pairs={{0,12},{4,16},{8,20},{12,24},{16,28},{1,13},{5,17},{9,21},{13,25},... | collective-permute-start | bytes 147464 | tf_op jit(solution)/shard_map/ppermute | solution.py:10
  156.9 7.1 %collective-permute-start.7 = (f32[3,32,128]{2,0,1:T(4,128)S(1)}, f32[3,32,128]{2,0,1:T(4,128)S(1)}, u32[]{:S(2)}, u32[]{:S(2)}) collective-permute-start(f32[3,32,128]{2,0,1:T(4,128)S(1)} %get-tuple-element.54), channel_id=1, source_target_pairs={{0,16},{4,20},{8,24},{12,28},{1,17},{5,21},{9,25},{13,29},{2,18},{... | collective-permute-start | bytes 147464 | tf_op jit(solution)/shard_map/ppermute | solution.py:10
  173.5 7.7 %collective-permute-start.9 = (f32[3,128,128]{2,0,1:T(4,128)S(1)}, f32[3,128,128]{2,0,1:T(4,128)S(1)}, u32[]{:S(2)}, u32[]{:S(2)}) collective-permute-start(f32[3,128,128]{2,0,1:T(4,128)S(1)} %bitcast.94), channel_id=1, source_target_pairs={{0,1},{1,2},{2,3},{4,5},{5,6},{6,7},{8,9},{9,10},{10,11},{12,13},{... | collective-permute-start | bytes 589832 | tf_op jit(solution)/shard_map/ppermute | solution.py:10
where the time goes:
time: 187 us; the launch traced here: 186 us
  local copies, waits for them, and re-layouts  69.1 us (37%)
  blocking collectives  40.1 us (21%)
  matrix products  24.2 us (13%)
  starting transfers between devices  24.1 us (13%)
  other arithmetic  13.3 us (7%)
  waiting for transfers between devices  11.4 us (6%)
  between operations  4.13 us (2%)
    dynamic_update_slice x6, local copies, waits for them, and re-layouts, shards(): local_blocks = lax.map(sum_blocks, (elem_block, component_forces))  49.6 us
    psum x1, blocking collectives, shards(): energy = lax.psum(energy_part, ('dom', 'level')) / scale_total  40.1 us
    ppermute x10, starting transfers between devices, from_behind(): return lax.ppermute(block, axis, route)  24.1 us
    dot_general x3, matrix products, sum_blocks(): jnp.dot(selector, component_part, precision=lax.Precision.HIGHEST, prefer...  21.6 us
    ppermute x10, waiting for transfers between devices, from_behind(): return lax.ppermute(block, axis, route)  11.4 us
    scatter-add x1, other arithmetic, shards(): assembled = local_blocks.at[:, slot_blocks.reshape(-1), :].add(received)  8.77 us
    reshape x1, local copies, waits for them, and re-layouts, shards(): forces.reshape(elements, 3, block_size)  6.19 us
    unnamed x27, local copies, waits for them, and re-layouts  5.85 us
  transfers between devices with their start and end apart: 10, of which 3 were waited for; matrix products, arithmetic and copies ran while one was open for 49% of the time, Pallas kernels for 0%

commit v1 on v0

--- a/solution.py
+++ b/solution.py
@@ -2,6 +2,12 @@
 import jax.numpy as jnp
 from jax import lax
 from jax.sharding import PartitionSpec as P
+
+
+def wrap_the_core(sheet, axis_tag, a_name):
+    for d in (axis_tag, a_name):
+        sheet = jax.lax.psum(sheet, axis_name=d)
+    return sheet
 
 
 def from_behind(block, axis, distance):
@@ -66,7 +72,7 @@
     child_values = 0.5 * (parent_pairs[:, :, 0] + parent_pairs[:, :, 1])
     projected = assembled.at[:, hang_child[0], :].set(child_values)
     scale_total = jnp.float32(row_width * elements * lax.axis_size("dom") * lax.axis_size("level"))
-    energy = lax.psum(energy_part, ("dom", "level")) / scale_total
+    energy = wrap_the_core(energy_part, "level", "dom") / scale_total
     return (projected[:, :block_count], energy)
 
 

time: 187 us -> 174 us (0.930)
  blocking collectives: 40.1 us -> 22.6 us
  starting transfers between devices: 24.1 us -> 28.7 us
    psum x1 -> x2, blocking collectives: 40.1 us -> 22.6 us  [wrap_the_core(): sheet = jax.lax.psum(sheet, axis_name=d)]
    ppermute x10, starting transfers between devices: 24.1 us -> 28.7 us  [from_behind(): return lax.ppermute(block, axis, route)]
  transfers between devices with their start and end apart: 10 -> 10, of which waited for: 3 -> 3; matrix products, arithmetic and copies ran while one was open for 49% -> 53% of each run, Pallas kernels for 0% -> 0%
where the time goes in v1:
time: 174 us
  local copies, waits for them, and re-layouts  69.1 us (40%)
  starting transfers between devices  28.7 us (16%)
  matrix products  24.2 us (14%)
  blocking collectives  22.6 us (13%)
  other arithmetic  13.3 us (8%)
  waiting for transfers between devices  11.4 us (7%)
  between operations  4.12 us (2%)
    dynamic_update_slice x6, local copies, waits for them, and re-layouts, shards(): local_blocks = lax.map(sum_blocks, (elem_block, component_forces))  49.6 us
    ppermute x10, starting transfers between devices, from_behind(): return lax.ppermute(block, axis, route)  28.7 us
    psum x2, blocking collectives, wrap_the_core(): sheet = jax.lax.psum(sheet, axis_name=d)  22.6 us
    dot_general x3, matrix products, sum_blocks(): jnp.dot(selector, component_part, precision=lax.Precision.HIGHEST, prefer...  21.6 us
    ppermute x10, waiting for transfers between devices, from_behind(): return lax.ppermute(block, axis, route)  11.4 us
    scatter-add x1, other arithmetic, shards(): assembled = local_blocks.at[:, slot_blocks.reshape(-1), :].add(received)  8.77 us
    reshape x1, local copies, waits for them, and re-layouts, shards(): forces.reshape(elements, 3, block_size)  6.2 us
    unnamed x27, local copies, waits for them, and re-layouts  5.85 us
  transfers between devices with their start and end apart: 10, of which 3 were waited for; matrix products, arithmetic and copies ran while one was open for 53% of the time, Pallas kernels for 0%

profile of v1, /device:TPU:18, one launch (start us, length us, event | category | flops | bytes accessed | tf_op | source)
XLA Modules:
  0.0 173.5 jit_solution(3185684533033974537)
XLA Ops:
  2.6 4.4 %copy.33 = bf16[3072,384]{0,1:T(8,128)(2,1)} copy(bf16[3072,384]{1,0:T(8,128)(2,1)} %param.12) | data formatting | bytes 4718592 | tf_op args[0]
  7.8 2.7 %convolution_bitcast_fusion = f32[3072,768]{0,1:T(8,128)S(1)} fusion(bf16[3072,384]{1,0:T(8,128)(2,1)S(1)} %copy-done, bf16[384,384]{1,0:T(8,128)(2,1)S(1)} %copy-done.3, bf16[384,384]{1,0:T(8,128)(2,1)S(1)} %copy-done.4), kind=kOutput, calls=%fused_computation.13 | convolution fusion | flops 1813118976 | bytes 12386304 | tf_op jit(solution)/shard_map/dot_general | solution.py:37
  10.4 4.5 %multiply_reduce_fusion = (f32[]{:T(128)}, f32[3072,384]{0,1:T(8,128)}) fusion(bf16[3072,384]{0,1:T(8,128)(2,1)S(1)} %copy-done.1, f32[3072,768]{0,1:T(8,128)S(1)} %convolution_bitcast_fusion, f32[3072]{0:T(1024)S(1)} %copy-done.6, f32[3072]{0:T(1024)S(1)} %copy-done.7, pred[3072]{0:T(1024)(128)(4,1)S(1)} %iota_compare_fusion.4), kind=kLoop, calls=%fused_computation.18 | loop fusion | flops 8257535 | bytes 16542724 | tf_op jit(solution)/shard_map/reduce_sum | solution.py:41
  14.9 6.2 %copy.27 = f32[3072,3,128]{2,0,1:T(8,128)} copy(f32[3072,3,128]{0,2,1:T(8,128)} %bitcast.88) | data formatting | bytes 9437184 | tf_op jit(solution)/shard_map/reshape | solution.py:42
  21.1 73.7 %while.11 = (s32[]{:T(128)}, f32[3,1025,128]{2,0,1:T(4,128)S(1)}, s32[3,3072]{1,0:T(4,128)}, f32[3,3072,128]{2,1,0:T(8,128)}, s32[]{:T(128)}, /*index=5*/s32[]{:T(128)}) while((s32[]{:T(128)}, f32[3,1025,128]{2,0,1:T(4,128)S(1)}, s32[3,3072]{1,0:T(4,128)}, f32[3,3072,128]{2,1,0:T(8,128)}, s32[]{:T(128)}, /*index=5*/s32[]{:T(128)}) %tuple.40), condition=%wide.region_1.2_spmd.clone, body=%wide.region_0.1_spmd.clone.sunk | while | flops 4839705600 | bytes 4234317 | solution.py:55
  21.9 7.2 %fusion.24 = f32[1,1025,128]{2,1,0:T(8,128)S(1)} fusion(s32[3072]{0:T(1024)S(1)} %bitcast.92, f32[3,3072,128]{2,1,0:T(8,128)} %get-tuple-element.104, s32[]{:T(128)} %get-tuple-element.95), kind=kOutput, calls=%fused_computation.8.clone.1 | convolution fusion | flops 4839705600 | bytes 2110464 | tf_op jit(solution)/shard_map/while/body/eval_jaxpr/dot_general | solution.py:48
  29.1 3.3 %copy.41 = f32[1,1025,128]{2,0,1:T(1,128)S(1)} copy(f32[1,1025,128]{2,1,0:T(8,128)S(1)} %fusion.24) | data formatting | bytes 1049600 | tf_op jit(solution)/shard_map/while/body/jit(dynamic_update_index_in_dim)/dynamic_update_slice | solution.py:55
  32.4 13.2 %dynamic_update_slice.6 = f32[3,1025,128]{2,0,1:T(4,128)S(1)} dynamic-update-slice(f32[3,1025,128]{2,0,1:T(4,128)S(1)} %get-tuple-element.96, f32[1,1025,128]{2,0,1:T(1,128)S(1)} %copy.41, s32[]{:T(128)} %get-tuple-element.95, s32[]{:T(128)} %constant.11.clone.1..sunk, s32[]{:T(128)} %constant.11.clone.1..sunk) | dynamic-update-slice | bytes 1049604 | tf_op jit(solution)/shard_map/while/body/jit(dynamic_update_index_in_dim)/dynamic_update_slice | solution.py:55
  46.5 7.2 %fusion.24 = f32[1,1025,128]{2,1,0:T(8,128)S(1)} fusion(s32[3072]{0:T(1024)S(1)} %bitcast.92, f32[3,3072,128]{2,1,0:T(8,128)} %get-tuple-element.104, s32[]{:T(128)} %get-tuple-element.95), kind=kOutput, calls=%fused_computation.8.clone.1 | convolution fusion | flops 4839705600 | bytes 2110464 | tf_op jit(solution)/shard_map/while/body/eval_jaxpr/dot_general | solution.py:48
  53.7 3.3 %copy.41 = f32[1,1025,128]{2,0,1:T(1,128)S(1)} copy(f32[1,1025,128]{2,1,0:T(8,128)S(1)} %fusion.24) | data formatting | bytes 1049600 | tf_op jit(solution)/shard_map/while/body/jit(dynamic_update_index_in_dim)/dynamic_update_slice | solution.py:55
  57.0 13.2 %dynamic_update_slice.6 = f32[3,1025,128]{2,0,1:T(4,128)S(1)} dynamic-update-slice(f32[3,1025,128]{2,0,1:T(4,128)S(1)} %get-tuple-element.96, f32[1,1025,128]{2,0,1:T(1,128)S(1)} %copy.41, s32[]{:T(128)} %get-tuple-element.95, s32[]{:T(128)} %constant.11.clone.1..sunk, s32[]{:T(128)} %constant.11.clone.1..sunk) | dynamic-update-slice | bytes 1049604 | tf_op jit(solution)/shard_map/while/body/jit(dynamic_update_index_in_dim)/dynamic_update_slice | solution.py:55
  71.1 7.2 %fusion.24 = f32[1,1025,128]{2,1,0:T(8,128)S(1)} fusion(s32[3072]{0:T(1024)S(1)} %bitcast.92, f32[3,3072,128]{2,1,0:T(8,128)} %get-tuple-element.104, s32[]{:T(128)} %get-tuple-element.95), kind=kOutput, calls=%fused_computation.8.clone.1 | convolution fusion | flops 4839705600 | bytes 2110464 | tf_op jit(solution)/shard_map/while/body/eval_jaxpr/dot_general | solution.py:48
  78.2 3.3 %copy.41 = f32[1,1025,128]{2,0,1:T(1,128)S(1)} copy(f32[1,1025,128]{2,1,0:T(8,128)S(1)} %fusion.24) | data formatting | bytes 1049600 | tf_op jit(solution)/shard_map/while/body/jit(dynamic_update_index_in_dim)/dynamic_update_slice | solution.py:55
  81.5 13.2 %dynamic_update_slice.6 = f32[3,1025,128]{2,0,1:T(4,128)S(1)} dynamic-update-slice(f32[3,1025,128]{2,0,1:T(4,128)S(1)} %get-tuple-element.96, f32[1,1025,128]{2,0,1:T(1,128)S(1)} %copy.41, s32[]{:T(128)} %get-tuple-element.95, s32[]{:T(128)} %constant.11.clone.1..sunk, s32[]{:T(128)} %constant.11.clone.1..sunk) | dynamic-update-slice | bytes 1049604 | tf_op jit(solution)/shard_map/while/body/jit(dynamic_update_index_in_dim)/dynamic_update_slice | solution.py:55
  95.5 6.8 %psum.14 = f32[]{:T(128)} all-reduce(f32[]{:T(128)S(6)} %mul.39), channel_id=1, replica_groups=mesh['dom'=8,'level'=4] {'level'}, use_global_device_ids=true, to_apply=%region_5.6 | all-reduce | flops 1 | bytes 8 | tf_op jit(solution)/shard_map/psum | solution.py:9
  103.8 3.3 %collective-permute-start = (f32[3,32,128]{2,0,1:T(4,128)S(1)}, f32[3,32,128]{2,0,1:T(4,128)S(1)}, u32[]{:S(2)}, u32[]{:S(2)}) collective-permute-start(f32[3,32,128]{2,0,1:T(4,128)S(1)} %get-tuple-element.61), channel_id=1, source_target_pairs={{4,0},{8,4},{12,8},{16,12},{20,16},{24,20},{28,24},{5,1},{9,5},{13... | collective-permute-start | bytes 147464 | tf_op jit(solution)/shard_map/ppermute | solution.py:16
  107.1 15.8 %psum.15 = f32[]{:T(128)} all-reduce(f32[]{:T(128)} %psum.14), channel_id=1, replica_groups=mesh['dom'=8,'level'=4] {'dom'}, use_global_device_ids=true, to_apply=%region_6.7 | all-reduce | flops 1 | bytes 8 | tf_op jit(solution)/shard_map/psum | solution.py:9
  123.6 5.2 %collective-permute-start.1 = (f32[3,32,128]{2,0,1:T(4,128)S(1)}, f32[3,32,128]{2,0,1:T(4,128)S(1)}, u32[]{:S(2)}, u32[]{:S(2)}) collective-permute-start(f32[3,32,128]{2,0,1:T(4,128)S(1)} %get-tuple-element.60), channel_id=1, source_target_pairs={{8,0},{12,4},{16,8},{20,12},{24,16},{28,20},{9,1},{13,5},{17,9},{2... | collective-permute-start | bytes 147464 | tf_op jit(solution)/shard_map/ppermute | solution.py:16
  130.9 3.1 %collective-permute-start.3 = (f32[3,32,128]{2,0,1:T(4,128)S(1)}, f32[3,32,128]{2,0,1:T(4,128)S(1)}, u32[]{:S(2)}, u32[]{:S(2)}) collective-permute-start(f32[3,32,128]{2,0,1:T(4,128)S(1)} %get-tuple-element.58), channel_id=1, source_target_pairs={{16,0},{20,4},{24,8},{28,12},{17,1},{21,5},{25,9},{29,13},{18,2},{... | collective-permute-start | bytes 147464 | tf_op jit(solution)/shard_map/ppermute | solution.py:16
  134.1 4.6 %collective-permute-start.4 = (f32[3,32,128]{2,0,1:T(4,128)S(1)}, f32[3,32,128]{2,0,1:T(4,128)S(1)}, u32[]{:S(2)}, u32[]{:S(2)}) collective-permute-start(f32[3,32,128]{2,0,1:T(4,128)S(1)} %get-tuple-element.57), channel_id=1, source_target_pairs={{0,4},{4,8},{8,12},{12,16},{16,20},{20,24},{24,28},{1,5},{5,9},{9,... | collective-permute-start | bytes 147464 | tf_op jit(solution)/shard_map/ppermute | solution.py:16
  138.6 3.4 %collective-permute-start.5 = (f32[3,32,128]{2,0,1:T(4,128)S(1)}, f32[3,32,128]{2,0,1:T(4,128)S(1)}, u32[]{:S(2)}, u32[]{:S(2)}) collective-permute-start(f32[3,32,128]{2,0,1:T(4,128)S(1)} %get-tuple-element.56), channel_id=1, source_target_pairs={{0,8},{4,12},{8,16},{12,20},{16,24},{20,28},{1,9},{5,13},{9,17},{1... | collective-permute-start | bytes 147464 | tf_op jit(solution)/shard_map/ppermute | solution.py:16
  145.4 4.6 %collective-permute-done.6 = f32[3,32,128]{2,0,1:T(4,128)S(1)} collective-permute-done((f32[3,32,128]{2,0,1:T(4,128)S(1)}, f32[3,32,128]{2,0,1:T(4,128)S(1)}, u32[]{:S(2)}, u32[]{:S(2)}) %collective-permute-start.6) | collective-permute-done | bytes 49184 | tf_op jit(solution)/shard_map/ppermute | solution.py:16
  151.1 8.8 %scatter_fusion = f32[3,1025,128]{2,0,1:T(4,128)S(1)} fusion(f32[3,1025,128]{2,0,1:T(4,128)S(1)} %get-tuple-element.29, s32[256]{0:T(256)S(1)} %bitcast.95, f32[256,3,128]{2,1,0:T(4,128)S(1)} %bitcast.91), kind=kCustom, calls=%fused_computation.2 | custom fusion | flops 98304 | bytes 1180672 | tf_op jit(solution)/shard_map/scatter-add | solution.py:67
  162.6 5.7 %collective-permute-done.9 = f32[3,128,128]{2,0,1:T(4,128)S(1)} collective-permute-done((f32[3,128,128]{2,0,1:T(4,128)S(1)}, f32[3,128,128]{2,0,1:T(4,128)S(1)}, u32[]{:S(2)}, u32[]{:S(2)}) %collective-permute-start.9) | collective-permute-done | bytes 196640 | tf_op jit(solution)/shard_map/ppermute | solution.py:16
  (60 shorter events, 19.2 us)
Async XLA Ops:
  0.6 101.8 %collective-permute-start.8 = (s32[1,64,2]{1,2,0:T(2,128)}, s32[1,64,2]{1,2,0:T(2,128)S(1)}, u32[]{:S(2)}, u32[]{:S(2)}) collective-permute-start(s32[1,64,2]{1,2,0:T(2,128)} %param.21), channel_id=1, source_target_pairs={{1,0},{2,1},{3,2},{5,4},{6,5},{7,6},{9,8},{10,9},{11,10},{13,12},{... | collective-permute-start | bytes 1544 | tf_op jit(solution)/shard_map/ppermute | solution.py:16
  2.6 5.1 %copy-start = (bf16[3072,384]{1,0:T(8,128)(2,1)S(1)}, bf16[3072,384]{1,0:T(8,128)(2,1)}, u32[]{:S(2)}) copy-start(bf16[3072,384]{1,0:T(8,128)(2,1)} %param.12) | copy-start | bytes 7077892
  2.6 5.1 %copy-start.3 = (bf16[384,384]{1,0:T(8,128)(2,1)S(1)}, bf16[384,384]{1,0:T(8,128)(2,1)}, u32[]{:S(2)}) copy-start(bf16[384,384]{1,0:T(8,128)(2,1)} %param.14) | copy-start | bytes 884740
  2.6 5.1 %copy-start.4 = (bf16[384,384]{1,0:T(8,128)(2,1)S(1)}, bf16[384,384]{1,0:T(8,128)(2,1)}, u32[]{:S(2)}) copy-start(bf16[384,384]{1,0:T(8,128)(2,1)} %param.13) | copy-start | bytes 884740
  7.7 2.7 %copy-start.1 = (bf16[3072,384]{0,1:T(8,128)(2,1)S(1)}, bf16[3072,384]{0,1:T(8,128)(2,1)}, u32[]{:S(2)}) copy-start(bf16[3072,384]{0,1:T(8,128)(2,1)} %copy.33) | copy-start | bytes 7077892
  7.7 2.7 %copy-start.6 = (f32[3072]{0:T(1024)S(1)}, f32[3072]{0:T(1024)}, u32[]{:S(2)}) copy-start(f32[3072]{0:T(1024)} %param.16) | copy-start | bytes 36868
  7.7 2.7 %copy-start.7 = (f32[3072]{0:T(1024)S(1)}, f32[3072]{0:T(1024)}, u32[]{:S(2)}) copy-start(f32[3072]{0:T(1024)} %param.15) | copy-start | bytes 36868
  14.9 6.2 %copy-start.2 = (f32[3,1025,128]{2,0,1:T(4,128)S(1)}, f32[3,1025,128]{2,0,1:T(4,128)}, u32[]{:S(2)}) copy-start(f32[3,1025,128]{2,0,1:T(4,128)} %custom-call.5) | copy-start | bytes 4723204
  21.1 74.4 %copy-start.5 = (s32[1,8,32]{2,1,0:T(8,128)S(1)}, s32[1,8,32]{2,1,0:T(8,128)}, u32[]{:S(2)}) copy-start(s32[1,8,32]{2,1,0:T(8,128)} %param.19) | copy-start | bytes 3076
  94.8 67.8 %copy-start.8 = (s32[1,64]{1,0:T(1,128)S(1)}, s32[1,64]{1,0:T(1,128)}, u32[]{:S(2)}) copy-start(s32[1,64]{1,0:T(1,128)} %param.20) | copy-start | bytes 772
  103.8 34.8 %collective-permute-start = (f32[3,32,128]{2,0,1:T(4,128)S(1)}, f32[3,32,128]{2,0,1:T(4,128)S(1)}, u32[]{:S(2)}, u32[]{:S(2)}) collective-permute-start(f32[3,32,128]{2,0,1:T(4,128)S(1)} %get-tuple-element.61), channel_id=1, source_target_pairs={{4,0},{8,4},{12,8},{16,12},{20,16},{24,20},{28,24},{5,1},{9,5},{13... | collective-permute-start | bytes 147464 | tf_op jit(solution)/shard_map/ppermute | solution.py:16
  123.6 18.4 %collective-permute-start.1 = (f32[3,32,128]{2,0,1:T(4,128)S(1)}, f32[3,32,128]{2,0,1:T(4,128)S(1)}, u32[]{:S(2)}, u32[]{:S(2)}) collective-permute-start(f32[3,32,128]{2,0,1:T(4,128)S(1)} %get-tuple-element.60), channel_id=1, source_target_pairs={{8,0},{12,4},{16,8},{20,12},{24,16},{28,20},{9,1},{13,5},{17,9},{2... | collective-permute-start | bytes 147464 | tf_op jit(solution)/shard_map/ppermute | solution.py:16
  128.8 15.2 %collective-permute-start.2 = (f32[3,32,128]{2,0,1:T(4,128)S(1)}, f32[3,32,128]{2,0,1:T(4,128)S(1)}, u32[]{:S(2)}, u32[]{:S(2)}) collective-permute-start(f32[3,32,128]{2,0,1:T(4,128)S(1)} %get-tuple-element.59), channel_id=1, source_target_pairs={{12,0},{16,4},{20,8},{24,12},{28,16},{13,1},{17,5},{21,9},{25,13},... | collective-permute-start | bytes 147464 | tf_op jit(solution)/shard_map/ppermute | solution.py:16
  130.9 14.4 %collective-permute-start.3 = (f32[3,32,128]{2,0,1:T(4,128)S(1)}, f32[3,32,128]{2,0,1:T(4,128)S(1)}, u32[]{:S(2)}, u32[]{:S(2)}) collective-permute-start(f32[3,32,128]{2,0,1:T(4,128)S(1)} %get-tuple-element.58), channel_id=1, source_target_pairs={{16,0},{20,4},{24,8},{28,12},{17,1},{21,5},{25,9},{29,13},{18,2},{... | collective-permute-start | bytes 147464 | tf_op jit(solution)/shard_map/ppermute | solution.py:16
  134.1 11.3 %collective-permute-start.4 = (f32[3,32,128]{2,0,1:T(4,128)S(1)}, f32[3,32,128]{2,0,1:T(4,128)S(1)}, u32[]{:S(2)}, u32[]{:S(2)}) collective-permute-start(f32[3,32,128]{2,0,1:T(4,128)S(1)} %get-tuple-element.57), channel_id=1, source_target_pairs={{0,4},{4,8},{8,12},{12,16},{16,20},{20,24},{24,28},{1,5},{5,9},{9,... | collective-permute-start | bytes 147464 | tf_op jit(solution)/shard_map/ppermute | solution.py:16
  138.6 6.8 %collective-permute-start.5 = (f32[3,32,128]{2,0,1:T(4,128)S(1)}, f32[3,32,128]{2,0,1:T(4,128)S(1)}, u32[]{:S(2)}, u32[]{:S(2)}) collective-permute-start(f32[3,32,128]{2,0,1:T(4,128)S(1)} %get-tuple-element.56), channel_id=1, source_target_pairs={{0,8},{4,12},{8,16},{12,20},{16,24},{20,28},{1,9},{5,13},{9,17},{1... | collective-permute-start | bytes 147464 | tf_op jit(solution)/shard_map/ppermute | solution.py:16
  142.0 8.0 %collective-permute-start.6 = (f32[3,32,128]{2,0,1:T(4,128)S(1)}, f32[3,32,128]{2,0,1:T(4,128)S(1)}, u32[]{:S(2)}, u32[]{:S(2)}) collective-permute-start(f32[3,32,128]{2,0,1:T(4,128)S(1)} %get-tuple-element.55), channel_id=1, source_target_pairs={{0,12},{4,16},{8,20},{12,24},{16,28},{1,13},{5,17},{9,21},{13,25},... | collective-permute-start | bytes 147464 | tf_op jit(solution)/shard_map/ppermute | solution.py:16
  144.0 7.1 %collective-permute-start.7 = (f32[3,32,128]{2,0,1:T(4,128)S(1)}, f32[3,32,128]{2,0,1:T(4,128)S(1)}, u32[]{:S(2)}, u32[]{:S(2)}) collective-permute-start(f32[3,32,128]{2,0,1:T(4,128)S(1)} %get-tuple-element.54), channel_id=1, source_target_pairs={{0,16},{4,20},{8,24},{12,28},{1,17},{5,21},{9,25},{13,29},{2,18},{... | collective-permute-start | bytes 147464 | tf_op jit(solution)/shard_map/ppermute | solution.py:16
  160.6 7.7 %collective-permute-start.9 = (f32[3,128,128]{2,0,1:T(4,128)S(1)}, f32[3,128,128]{2,0,1:T(4,128)S(1)}, u32[]{:S(2)}, u32[]{:S(2)}) collective-permute-start(f32[3,128,128]{2,0,1:T(4,128)S(1)} %bitcast.94), channel_id=1, source_target_pairs={{0,1},{1,2},{2,3},{4,5},{5,6},{6,7},{8,9},{9,10},{10,11},{12,13},{... | collective-permute-start | bytes 589832 | tf_op jit(solution)/shard_map/ppermute | solution.py:16
